TPU v7x, 16 devices: a 4x2x1 block of a 4x4x8 slice. The times are simulated.
16 devices in a mesh: dp: 2 (over y, z), tp: 8 (over x, core).
Axes of the slice: x: 4, y: 2, z: 1, core: 2. Of those that a mesh axis runs over, the one named last changes fastest.
The devices are a block of a 4x4x8 slice.
Arguments:
- x: bfloat16 [8, 2048, 5120], P('dp'), parts along dimension 0
- gamma: float32 [5120], replicated
- beta: float32 [5120], replicated
- wqkv: bfloat16 [5120, 15360], P(None, 'tp')
- wo: bfloat16 [40, 128, 5120], P('tp')
- w1: bfloat16 [5120, 20480], P(None, 'tp')
- w2: bfloat16 [20480, 5120], P('tp')
Outputs:
- output: bfloat16 [8, 2048, 5120], P('dp'), parts along dimension 0
There are 2 independent parts. A program takes and returns all parts, laid end to end along the dimension named above; an argument that names none is the same for every part.
All inputs are finite; a program needn't handle non-finite values.
Results may differ from a plain program's by a relative error of at most 0.0104394.
Values are sent between devices in bfloat16 or wider.
A program may use at most 768 MiB of HBM per device.

v0:
```python
import functools
import jax
import jax.numpy as jnp
from jax import lax
from jax.sharding import PartitionSpec as P


def layer_norm(x, gamma, beta):
    xf = x.astype(jnp.float32)
    mu = jnp.mean(xf, axis=-1, keepdims=True)
    var = jnp.mean(jnp.square(xf - mu), axis=-1, keepdims=True)
    return ((xf - mu) * lax.rsqrt(var + 1e-5) * gamma + beta).astype(jnp.bfloat16)


def attend(qkv_b, hpg):
    s = qkv_b.shape[0]
    dh = qkv_b.shape[-1]
    q = qkv_b[:, :, :hpg]
    k = qkv_b[:, :, hpg]
    v = qkv_b[:, :, hpg + 1]
    sc = jnp.einsum('sghd,tgd->ghst', q, k, preferred_element_type=jnp.float32) * (dh ** -0.5)
    pos = jnp.arange(s)
    sc = jnp.where((pos[:, None] >= pos[None, :])[None, None], sc, -1e30)
    p = jax.nn.softmax(sc, axis=-1).astype(jnp.bfloat16)
    o = jnp.einsum('ghst,tgd->sghd', p, v, preferred_element_type=jnp.float32)
    return o.astype(jnp.bfloat16).reshape(s, -1)


def solution(mesh):
    def local(x, gamma, beta, wqkv, wo, w1, w2):
        b, s, d = x.shape
        hl, dh, _ = wo.shape
        gl = (wqkv.shape[1] - hl * dh) // (2 * dh)
        hpg = hl // gl
        ntok = b * s
        ln = layer_norm(x, gamma, beta).reshape(ntok, d)
        qkv = jnp.dot(ln, wqkv, preferred_element_type=jnp.float32).astype(jnp.bfloat16)
        o = lax.map(functools.partial(attend, hpg=hpg), qkv.reshape(b, s, gl, hpg + 2, dh))
        a = jnp.dot(o.reshape(ntok, hl * dh), wo.reshape(hl * dh, d), preferred_element_type=jnp.float32)
        hmid = jax.nn.gelu(jnp.dot(ln, w1, preferred_element_type=jnp.float32), approximate=False).astype(jnp.bfloat16)
        part_sum = (a + jnp.dot(hmid, w2, preferred_element_type=jnp.float32)).astype(jnp.bfloat16)
        total = lax.psum(part_sum, 'tp')
        return (x.astype(jnp.float32) + total.astype(jnp.float32).reshape(b, s, d)).astype(jnp.bfloat16)

    return jax.shard_map(local, mesh=mesh,
                         in_specs=(P('dp', None, None), P(None), P(None), P(None, 'tp'),
                                   P('tp', None, None), P(None, 'tp'), P('tp', None)),
                         out_specs=P('dp', None, None), check_vma=False)
```

profile of v0, /device:TPU:112, one launch (start us, length us, event | category | flops | bytes accessed | tf_op | source)
XLA Modules:
  0.0 2484.0 jit_solution(14628168391182421574)
XLA Ops:
  6.5 0.0 all-reduce.2.cloned.1.call-start
  6.6 0.0 copy-start
  6.6 0.0 copy-start.1
  6.6 25.9 %convert_reduce_fusion = f32[4,2048]{1,0:T(4,128)S(1)} fusion(bf16[4,2048,5120]{2,1,0:T(8,128)(2,1)} %param.9), kind=kLoop, calls=%fused_computation.19 | loop fusion | flops 83877888 | bytes 83918848 | tf_op jit(solution)/shard_map/reduce_sum | solution.py:10
  32.5 30.1 %fusion.12 = f32[4,2048]{1,0:T(4,128)S(1)} fusion(bf16[4,2048,5120]{2,1,0:T(8,128)(2,1)} %param.9, f32[4,2048]{1,0:T(4,128)S(1)} %broadcast_multiply_fusion), kind=kLoop, calls=%fused_computation.22 | loop fusion | flops 167763968 | bytes 83951616 | tf_op jit(solution)/shard_map/reduce_sum | solution.py:11
  62.6 0.0 copy-done
  62.6 0.0 copy-done.1
  62.6 55.7 %fusion.15 = bf16[4,2048,5120]{2,1,0:T(8,128)(2,1)} fusion(bf16[4,2048,5120]{2,1,0:T(8,128)(2,1)} %param.9, f32[5120]{0:T(1024)S(1)} %copy-done, f32[5120]{0:T(1024)S(1)} %copy-done.1, f32[4,2048]{1,0:T(4,128)S(1)} %add_rsqrt_fusion, f32[4,2048]{1,0:T(4,128)S(1)} %broadcast_multiply_fusion), kind=kLoop, calls=%fused_computation.25 | loop fusion | flops 251658240 | bytes 167878656 | tf_op jit(solution)/shard_map/convert_element_type | solution.py:12
  118.3 185.7 %convolution_convert_fusion = bf16[8192,1920]{1,0:T(8,128)(2,1)} fusion(bf16[8192,5120]{1,0:T(8,128)(2,1)} %bitcast.10, bf16[5120,1920]{1,0:T(8,128)(2,1)} %param.12), kind=kOutput, calls=%fused_computation.78 | convolution fusion | flops 161077002240 | bytes 135004160 | tf_op jit(solution)/shard_map/dot_general | solution.py:37
  304.0 229.4 %fusion.89 = f32[8192,2560]{1,0:T(8,128)} fusion(bf16[8192,5120]{1,0:T(8,128)(2,1)} %bitcast.10, bf16[5120,2560]{1,0:T(8,128)(2,1)} %param.14), kind=kOutput, calls=%fused_computation.111 | convolution fusion | flops 214748364800 | bytes 193986560 | tf_op jit(solution)/shard_map/dot_general | solution.py:40
  533.4 75.7 %reshape.75 = bf16[4,2048,5,3,128]{4,3,2,1,0:T(4,128)(2,1)} reshape(bf16[8192,1920]{1,0:T(8,128)(2,1)} %convolution_convert_fusion) | data formatting | bytes 62914560 | tf_op jit(solution)/shard_map/reshape | solution.py:38
  609.1 25.1 %copy.14 = bf16[4,2048,5,3,128]{4,1,2,3,0:T(8,128)(2,1)} copy(bf16[4,2048,5,3,128]{4,3,2,1,0:T(4,128)(2,1)} %reshape.75) | data formatting | bytes 62914560 | tf_op jit(solution)/shard_map/while | solution.py:38
  634.2 453.9 %while.10 = (s32[]{:T(128)}, bf16[4,2048,640]{2,1,0:T(8,128)(2,1)}, bf16[4,2048,5,3,128]{4,1,2,3,0:T(8,128)(2,1)}, s32[]{:T(128)}) while((s32[]{:T(128)}, bf16[4,2048,640]{2,1,0:T(8,128)(2,1)}, bf16[4,2048,5,3,128]{4,1,2,3,0:T(8,128)(2,1)}, s32[]{:T(128)}) %tuple.23), condition=%wide.region_5.6_spmd, body=%wide.region_2.5_spmd.sunk | while | flops 10994561024 | bytes 305340480 | solution.py:38
  634.5 4.1 iota_compare_fusion.2
  638.6 7.1 dynamic-slice_bitcast_fusion.2
  645.7 33.1 %fusion.105 = (f32[5,2048]{1,0:T(8,128)S(1)}, f32[5,2048,2048]{2,1,0:T(8,128)}) fusion(pred[2048,2048]{0,1:T(8,128)(4,1)} %iota_compare_fusion.2, bf16[2048,5,3,128]{3,0,1,2:T(8,128)(2,1)} %dynamic-slice_bitcast_fusion.2), kind=kOutput, calls=%fused_computation.4.clone.1 | convolution fusion | flops 5431613440 | bytes 93364224 | tf_op jit(solution)/shard_map/while/body/eval_jaxpr/sghd,tgd->ghst/dot_general | solution.py:21
  678.9 27.7 %fusion.106 = f32[5,2048]{1,0:T(8,128)S(1)} fusion(f32[5,2048,2048]{2,1,0:T(8,128)} %get-tuple-element.58, f32[5,2048]{1,0:T(8,128)S(1)} %get-tuple-element.59, pred[2048,2048]{0,1:T(8,128)(4,1)} %iota_compare_fusion.2), kind=kLoop, calls=%fused_computation.3.clone.1 | loop fusion | flops 83875840 | bytes 88162304 | tf_op jit(solution)/shard_map/while/body/eval_jaxpr/reduce_sum | solution.py:24
  706.6 36.5 %fusion.107 = bf16[5,128,2048]{2,1,0:T(8,128)(2,1)} fusion(f32[5,2048]{1,0:T(8,128)S(1)} %fusion.106, f32[5,2048]{1,0:T(8,128)S(1)} %get-tuple-element.59, f32[5,2048,2048]{2,1,0:T(8,128)} %get-tuple-element.58, pred[2048,2048]{0,1:T(8,128)(4,1)} %iota_compare_fusion.2, bf16[2048,5,3,128]{3,0,1,2:T(8,128)(2,1)} %dynamic-slice_bitcast_fusion.2), kind=kOutput, calls=%fused_computation.9.clone.1 | convolution fusion | flops 5474877440 | bytes 93405184 | tf_op jit(solution)/shard_map/while/body/eval_jaxpr/ghst,tgd->sghd/dot_general | solution.py:25
  743.1 3.1 copy.23
  746.2 1.7 constant_dynamic-update-slice_fusion.2
  747.9 4.1 iota_compare_fusion.2
  752.0 7.1 dynamic-slice_bitcast_fusion.2
  759.1 33.1 %fusion.105 = (f32[5,2048]{1,0:T(8,128)S(1)}, f32[5,2048,2048]{2,1,0:T(8,128)}) fusion(pred[2048,2048]{0,1:T(8,128)(4,1)} %iota_compare_fusion.2, bf16[2048,5,3,128]{3,0,1,2:T(8,128)(2,1)} %dynamic-slice_bitcast_fusion.2), kind=kOutput, calls=%fused_computation.4.clone.1 | convolution fusion | flops 5431613440 | bytes 93364224 | tf_op jit(solution)/shard_map/while/body/eval_jaxpr/sghd,tgd->ghst/dot_general | solution.py:21
  792.2 27.7 %fusion.106 = f32[5,2048]{1,0:T(8,128)S(1)} fusion(f32[5,2048,2048]{2,1,0:T(8,128)} %get-tuple-element.58, f32[5,2048]{1,0:T(8,128)S(1)} %get-tuple-element.59, pred[2048,2048]{0,1:T(8,128)(4,1)} %iota_compare_fusion.2), kind=kLoop, calls=%fused_computation.3.clone.1 | loop fusion | flops 83875840 | bytes 88162304 | tf_op jit(solution)/shard_map/while/body/eval_jaxpr/reduce_sum | solution.py:24
  820.0 36.5 %fusion.107 = bf16[5,128,2048]{2,1,0:T(8,128)(2,1)} fusion(f32[5,2048]{1,0:T(8,128)S(1)} %fusion.106, f32[5,2048]{1,0:T(8,128)S(1)} %get-tuple-element.59, f32[5,2048,2048]{2,1,0:T(8,128)} %get-tuple-element.58, pred[2048,2048]{0,1:T(8,128)(4,1)} %iota_compare_fusion.2, bf16[2048,5,3,128]{3,0,1,2:T(8,128)(2,1)} %dynamic-slice_bitcast_fusion.2), kind=kOutput, calls=%fused_computation.9.clone.1 | convolution fusion | flops 5474877440 | bytes 93405184 | tf_op jit(solution)/shard_map/while/body/eval_jaxpr/ghst,tgd->sghd/dot_general | solution.py:25
  856.4 3.1 copy.23
  859.6 1.7 constant_dynamic-update-slice_fusion.2
  861.3 4.1 iota_compare_fusion.2
  865.4 7.1 dynamic-slice_bitcast_fusion.2
  872.5 33.2 %fusion.105 = (f32[5,2048]{1,0:T(8,128)S(1)}, f32[5,2048,2048]{2,1,0:T(8,128)}) fusion(pred[2048,2048]{0,1:T(8,128)(4,1)} %iota_compare_fusion.2, bf16[2048,5,3,128]{3,0,1,2:T(8,128)(2,1)} %dynamic-slice_bitcast_fusion.2), kind=kOutput, calls=%fused_computation.4.clone.1 | convolution fusion | flops 5431613440 | bytes 93364224 | tf_op jit(solution)/shard_map/while/body/eval_jaxpr/sghd,tgd->ghst/dot_general | solution.py:21
  905.6 27.7 %fusion.106 = f32[5,2048]{1,0:T(8,128)S(1)} fusion(f32[5,2048,2048]{2,1,0:T(8,128)} %get-tuple-element.58, f32[5,2048]{1,0:T(8,128)S(1)} %get-tuple-element.59, pred[2048,2048]{0,1:T(8,128)(4,1)} %iota_compare_fusion.2), kind=kLoop, calls=%fused_computation.3.clone.1 | loop fusion | flops 83875840 | bytes 88162304 | tf_op jit(solution)/shard_map/while/body/eval_jaxpr/reduce_sum | solution.py:24
  933.4 36.5 %fusion.107 = bf16[5,128,2048]{2,1,0:T(8,128)(2,1)} fusion(f32[5,2048]{1,0:T(8,128)S(1)} %fusion.106, f32[5,2048]{1,0:T(8,128)S(1)} %get-tuple-element.59, f32[5,2048,2048]{2,1,0:T(8,128)} %get-tuple-element.58, pred[2048,2048]{0,1:T(8,128)(4,1)} %iota_compare_fusion.2, bf16[2048,5,3,128]{3,0,1,2:T(8,128)(2,1)} %dynamic-slice_bitcast_fusion.2), kind=kOutput, calls=%fused_computation.9.clone.1 | convolution fusion | flops 5474877440 | bytes 93405184 | tf_op jit(solution)/shard_map/while/body/eval_jaxpr/ghst,tgd->sghd/dot_general | solution.py:25
  969.8 3.1 copy.23
  972.9 1.7 constant_dynamic-update-slice_fusion.2
  974.7 4.1 iota_compare_fusion.2
  978.8 7.1 dynamic-slice_bitcast_fusion.2
  985.9 33.1 %fusion.105 = (f32[5,2048]{1,0:T(8,128)S(1)}, f32[5,2048,2048]{2,1,0:T(8,128)}) fusion(pred[2048,2048]{0,1:T(8,128)(4,1)} %iota_compare_fusion.2, bf16[2048,5,3,128]{3,0,1,2:T(8,128)(2,1)} %dynamic-slice_bitcast_fusion.2), kind=kOutput, calls=%fused_computation.4.clone.1 | convolution fusion | flops 5431613440 | bytes 93364224 | tf_op jit(solution)/shard_map/while/body/eval_jaxpr/sghd,tgd->ghst/dot_general | solution.py:21
  1019.0 27.7 %fusion.106 = f32[5,2048]{1,0:T(8,128)S(1)} fusion(f32[5,2048,2048]{2,1,0:T(8,128)} %get-tuple-element.58, f32[5,2048]{1,0:T(8,128)S(1)} %get-tuple-element.59, pred[2048,2048]{0,1:T(8,128)(4,1)} %iota_compare_fusion.2), kind=kLoop, calls=%fused_computation.3.clone.1 | loop fusion | flops 83875840 | bytes 88162304 | tf_op jit(solution)/shard_map/while/body/eval_jaxpr/reduce_sum | solution.py:24
  1046.7 36.5 %fusion.107 = bf16[5,128,2048]{2,1,0:T(8,128)(2,1)} fusion(f32[5,2048]{1,0:T(8,128)S(1)} %fusion.106, f32[5,2048]{1,0:T(8,128)S(1)} %get-tuple-element.59, f32[5,2048,2048]{2,1,0:T(8,128)} %get-tuple-element.58, pred[2048,2048]{0,1:T(8,128)(4,1)} %iota_compare_fusion.2, bf16[2048,5,3,128]{3,0,1,2:T(8,128)(2,1)} %dynamic-slice_bitcast_fusion.2), kind=kOutput, calls=%fused_computation.9.clone.1 | convolution fusion | flops 5474877440 | bytes 93405184 | tf_op jit(solution)/shard_map/while/body/eval_jaxpr/ghst,tgd->sghd/dot_general | solution.py:25
  1083.2 3.1 copy.23
  1086.3 1.7 constant_dynamic-update-slice_fusion.2
  1088.1 397.1 %fusion.27 = f32[8192,5120]{1,0:T(8,128)} fusion(bf16[2560,5120]{1,0:T(8,128)(2,1)} %param.15, f32[8192,2560]{1,0:T(8,128)} %fusion.89), kind=kOutput, calls=%fused_computation.47 | convolution fusion | flops 216111513600 | bytes 277872640 | tf_op jit(solution)/shard_map/dot_general | solution.py:41
  1485.1 103.3 %add_convert_fusion = bf16[8192,5120]{1,0:T(8,128)(2,1)} fusion(f32[8192,5120]{1,0:T(8,128)} %fusion.27, bf16[8192,640]{1,0:T(8,128)(2,1)} %bitcast.71, bf16[640,5120]{1,0:T(8,128)(2,1)} %bitcast.72), kind=kOutput, calls=%fused_computation.27 | convolution fusion | flops 53770977280 | bytes 268697600 | tf_op jit(solution)/shard_map/dot_general | solution.py:39
  1588.4 0.1 all-reduce.2.cloned.1.call-update
  1588.5 807.7 %all-reduce.2.cloned.1.call-done = bf16[4,2048,5120]{2,1,0:T(8,128)(2,1)} async-done(((bf16[4,2048,5120]{2,1,0:T(8,128)(2,1)}), bf16[4,2048,5120]{2,1,0:T(8,128)(2,1)}) %all-reduce.2.cloned.1.call-update) | async-done | bytes 83886096 | tf_op jit(solution)/shard_map/psum | solution.py:42
  2396.1 80.7 %fusion.16 = bf16[4,2048,5120]{2,1,0:T(8,128)(2,1)} fusion(bf16[4,2048,5120]{2,1,0:T(8,128)(2,1)} %param.9, bf16[4,2048,5120]{2,1,0:T(8,128)(2,1)} %all-reduce.2.cloned.1.call-done), kind=kLoop, calls=%fused_computation.26 | loop fusion | flops 167772160 | bytes 251658240 | tf_op jit(solution)/shard_map/convert_element_type | solution.py:43
  (3 shorter events, 0.0 us)
Async XLA Ops:
  6.5 2389.6 %all-reduce.2.cloned.1.call-start = ((), (), s32[]{:S(2)}) async-start(), calls=%async_computation | async-start | bytes 167772160 | tf_op jit(solution)/shard_map/psum | solution.py:42
  6.6 56.0 %copy-start = (f32[5120]{0:T(1024)S(1)}, f32[5120]{0:T(1024)}, u32[]{:S(2)}) copy-start(f32[5120]{0:T(1024)} %param.11) | copy-start | bytes 61444
  6.6 56.1 %copy-start.1 = (f32[5120]{0:T(1024)S(1)}, f32[5120]{0:T(1024)}, u32[]{:S(2)}) copy-start(f32[5120]{0:T(1024)} %param.10) | copy-start | bytes 61444
Sparse Core Ops, SparseCore 0:
  1588.6 807.4 all-reduce.1
where the time goes:
time: 2490 us; the launch traced here: 2480 us
  matrix products  1190 us (48%)
  waiting for transfers between devices  808 us (32%)
  other arithmetic  320 us (13%)
  local copies, waits for them, and re-layouts  149 us (6%)
    psum x1, waiting for transfers between devices, local(): total = lax.psum(part_sum, 'tp')  808 us
    dot_general x1, matrix products, local(): jnp.dot(hmid, w2, preferred_element_type=jnp.float32)  397 us
    dot_general x1, matrix products, local(): jnp.dot(ln, w1, preferred_element_type=jnp.float32)  229 us
    dot_general x1, matrix products, local(): jnp.dot(ln, wqkv, preferred_element_type=jnp.float32).astype(jnp.bfloat16)  186 us
    dot_general x4, matrix products, attend(): o = jnp.einsum('ghst,tgd->sghd', p, v, preferred_element_type=jnp.float32)  146 us
    dot_general x4, matrix products, attend(): jnp.einsum('sghd,tgd->ghst', q, k, preferred_element_type=jnp.float32)  133 us
    reduce_sum x4, other arithmetic, attend(): p = jax.nn.softmax(sc, axis=-1).astype(jnp.bfloat16)  111 us
    dot_general x1, matrix products, local(): jnp.dot(o.reshape(ntok, hl * dh), wo.reshape(hl * dh, d), preferred_eleme...  103 us
  transfers between devices with their start and end apart: 1, of which 1 were waited for; matrix products, arithmetic and copies ran while one was open for 0% of the time, Pallas kernels for 0%

commit v1 on v0

v1 whole, which is shorter than its diff:
```python
import functools
import math

import jax
import jax.numpy as jnp
from jax import lax
from jax.experimental import pallas as pl
from jax.experimental.pallas import tpu as pltpu
from jax.sharding import PartitionSpec as P

BF = jnp.bfloat16
F32 = jnp.float32
DEPTH = 4
RING = 10
LAST = 11
CHANNELS = 13
COMM = True


def kernel(cfg, x, gamma, beta, wqkv, wo, w1, w2, y,
           wbuf, ln, qb, kc, vc, hbuf, part, xbuf, sb0, sb1, pb, mt0, mt1, s1r, r1l, r1r, r2l, r2r, ybuf, xp,
           wsem, xsem, ssem, rsem, ysem, xpsem):
    (ntok, d, s, hl, dh, f, tc, tp) = cfg
    sb, mt = (sb0, sb1), (mt0, mt1)
    hd = hl * dh
    chunks, per_seq = ntok // tc, s // tc
    nk = 8
    nb, dw, gw = d // nk, d // 4, f // 2
    qw = 3 * hd
    qa = (qw // 2 + 255) // 256 * 256
    th, to = tc // 2, tc // tp
    half = to // 2
    lnr = tc // 4
    nblk = chunks * nk
    nx = tp // 2

    me = lax.axis_index("tp")
    cx, q = me // 2, me % 2
    right = {"tp": ((cx + 1) % nx) * 2 + q}
    left = {"tp": ((cx + nx - 1) % nx) * 2 + q}
    partner = {"tp": cx * 2 + 1 - q}
    o_me = q * th + cx * to
    o_right = q * th + ((cx + 1) % nx) * to
    o_left = q * th + ((cx + nx - 1) % nx) * to
    o_opp = q * th + ((cx + 2) % nx) * to
    mine, theirs = q * th, (1 - q) * th

    def rows(start, size):
        return pl.ds(pl.multiple_of(start, math.gcd(size, half)), size)

    def wload(step, slot, i=None):
        if step == "q0":
            return [pltpu.make_async_copy(wqkv.at[:, 0:qa], wbuf.at[slot, 0:d, 0:qa], wsem.at[slot, 0])]
        if step == "q1":
            return [pltpu.make_async_copy(wqkv.at[:, qa:qw], wbuf.at[slot, 0:d, 0:qw - qa], wsem.at[slot, 0])]
        if step == "g":
            return [pltpu.make_async_copy(w1.at[:, pl.ds(pl.multiple_of(i * gw, 128), gw)], wbuf.at[slot, 0:d, 0:gw], wsem.at[slot, 0])]
        cols = pl.ds(pl.multiple_of(i * dw, 128), dw)
        return [pltpu.make_async_copy(w2.at[:, cols], wbuf.at[slot, 0:f, 0:dw], wsem.at[slot, 0]),
                pltpu.make_async_copy(wo.at[:, cols], wbuf.at[slot, f:f + hd, 0:dw], wsem.at[slot, 1])]

    def start(copies):
        for copy in copies:
            copy.start()

    def wait(copies):
        for copy in copies:
            copy.wait()

    def gather(tiles):
        return jnp.concatenate([tiles[:, g].reshape(tc, 128) for g in range(tiles.shape[1])], axis=1)

    def scatter(tiles, first, val):
        for g in range(val.shape[1] // 128):
            tiles[:, first + g] = val[:, g * 128:(g + 1) * 128].reshape(tc // 16, 16, 128)

    def xload(c, i):
        return pltpu.make_async_copy(x.at[pl.ds(pl.multiple_of(c * tc + i * lnr, lnr), lnr), :], xbuf.at[i % 2], xsem.at[i % 2])

    def norm(i):
        sub = 16
        for r in range(lnr // sub):
            xs = xbuf[i % 2, r * sub:(r + 1) * sub, :].astype(F32)
            xc = xs - jnp.sum(xs, axis=-1, keepdims=True) * (1.0 / d)
            inv = lax.rsqrt(jnp.sum(xc * xc, axis=-1, keepdims=True) * (1.0 / d) + 1e-5)
            out = (xc * inv * gamma[...] + beta[...]).astype(BF)
            for g in range(d // 128):
                ln[i * (lnr // sub) + r, g] = out[:, g * 128:(g + 1) * 128]

    def k(b):
        return lax.rem(b + 16, DEPTH)

    def ring(b):
        return lax.rem(b + 2 * RING, RING)

    def safe(b, i, spare):
        return jnp.where(b >= 0, i, spare)

    def y_at(b, off, size):
        c, kk = b // nk, b % nk
        return y.at[rows(c * tc + off, size), pl.ds(pl.multiple_of(kk * nb, 128), nb)]

    def remote(ch, b, src, dst, dev):
        return pltpu.make_async_remote_copy(src, dst, ssem.at[ch, k(b)], rsem.at[ch, k(b)], device_id=dev, device_id_type=pl.DeviceIdType.MESH)

    def t_pair(b):
        return [remote(0, b, part.at[ring(b), rows(theirs, th), :], s1r.at[lax.rem(b + 16, 2)], partner)]

    def t_first(b):
        p = ring(b)
        return [remote(1, b, part.at[p, rows(o_opp, half), :], r1l.at[k(b)], right),
                remote(2, b, part.at[p, rows(o_opp + half, half), :], r1r.at[k(b)], left)]

    def t_second(b):
        p = ring(b)
        return [remote(3, b, part.at[p, rows(o_right, to), :], r2l.at[k(b)], right),
                remote(4, b, part.at[p, rows(o_left, to), :], r2r.at[k(b)], left)]

    def t_own(b):
        src, dst = ybuf.at[k(b)], y_at(b, o_me, to)
        return [remote(5, b, src, dst, right), remote(6, b, src, dst, left), remote(7, b, src, dst, partner)]

    def t_keep(b):
        return pltpu.make_async_copy(ybuf.at[k(b)], y_at(b, o_me, to), ysem.at[k(b)])

    def t_pass(b):
        a, z = y_at(b, o_left, half), y_at(b, o_right + half, half)
        l, r = y_at(b, o_left, to), y_at(b, o_right, to)
        return [remote(8, b, a, a, right), remote(9, b, z, z, left), remote(10, b, l, l, partner), remote(11, b, r, r, partner)]

    def t_opp(b):
        o = y_at(b, o_opp, to)
        return [remote(12, b, o, o, partner)]

    def t_x(b):
        c, kk = b // nk, b % nk
        return pltpu.make_async_copy(x.at[rows(c * tc + o_me, to), pl.ds(pl.multiple_of(kk * nb, 128), nb)], xp.at[k(b)], xpsem.at[k(b)])

    def drain(copies):
        for copy in copies:
            copy.wait_recv()
            copy.wait_send()

    def waits(n, on):
        on(n - 1, lambda b: drain(t_pair(b)))
        on(n - 3, lambda b: drain(t_first(b)))
        on(n - 5, lambda b: (drain(t_second(b)), t_x(b).wait()))
        on(n - 7, lambda b: (drain(t_own(b)), t_keep(b).wait()))
        on(n - 9, lambda b: drain(t_pass(b)))
        on(n - LAST, lambda b: drain(t_opp(b)))

    def sends(n, on):
        on(n - 9, lambda b: start(t_opp(b)))
        on(n - 7, lambda b: start(t_pass(b)))
        on(n - 5, lambda b: (start(t_own(b)), t_keep(b).start()))
        on(n - 3, lambda b: (start(t_second(b)), t_x(b).start()))
        on(n - 1, lambda b: start(t_first(b)))
        on(n, lambda b: start(t_pair(b)))

    def sum_pair(b, p, i):
        at = rows(mine, th)
        part[p, at, :] = part[p, at, :] + s1r[i]

    def sum_first(b, p, i):
        at = rows(o_right, half)
        part[p, at, :] = part[p, at, :] + r1l[i]
        at = rows(o_left + half, half)
        part[p, at, :] = part[p, at, :] + r1r[i]

    def sum_second(b, p, i):
        u = part[p, rows(o_me, to), :].astype(F32) + (r2l[i].astype(F32) + r2r[i].astype(F32))
        ybuf[k(b)] = (xp[i].astype(F32) + u.astype(BF).astype(F32)).astype(BF)

    def adds(n):
        for delta, f_ in ((1, sum_pair), (3, sum_first), (5, sum_second)):
            b = n - delta
            f_(b, ring(b), safe(b, lax.rem(b + 16, 2), 2) if delta == 1 else safe(b, k(b), DEPTH))

    def guarded(cond, b, g):
        @pl.when(cond)
        def _():
            g(b)

    def when_at_least(n, f_):
        hot = n >= LAST

        @pl.when(hot)
        def _():
            f_(n, lambda b, g: g(b))

        @pl.when(jnp.logical_not(hot))
        def _():
            f_(n, lambda b, g: guarded(b >= 0, b, g))

    def step(n, compute):
        if COMM:
            when_at_least(n, waits)
            adds(n)
        compute()
        if COMM:
            when_at_least(n, sends)

    def put_qkv(c, r, first):
        base = pl.multiple_of(lax.rem(c, per_seq) * tc, tc)
        for i in range(r.shape[1] // dh):
            head, kind = divmod(first // dh + i, 3)
            val = r[:, i * dh:(i + 1) * dh].astype(BF)
            if kind == 0:
                qb[head] = val
            else:
                (kc, vc)[kind - 1][head, pl.ds(base, tc), :] = val

    def attend(c):
        scale = dh ** -0.5 * math.log2(math.e)
        j = lax.rem(c, per_seq)
        qr = tc // 2
        block = min(64, qr)
        blocks = [slice(r, r + block) for r in range(0, qr, block)]

        def scores(h, i, tiles):
            width = (tiles - 1) * tc + (i + 1) * qr
            m = None
            for lo in range(0, width, tc):
                hi = min(lo + tc, width)
                st = lax.dot_general(qb[h, i * qr:(i + 1) * qr, :], kc[h, lo:hi, :], (((1,), (1,)), ((), ())), preferred_element_type=F32)
                if hi == width:
                    row = lax.broadcasted_iota(jnp.int32, st.shape, 0) + i * qr
                    st = jnp.where(row >= lax.broadcasted_iota(jnp.int32, st.shape, 1), st, -1e30)
                sb[i][:, lo:hi] = st
                for g in range(0, hi - lo, 128):
                    v = st[:, g:g + 128]
                    m = v if m is None else jnp.maximum(m, v)
            mt[i][...] = m

        def output(h, i, tiles):
            width = (tiles - 1) * tc + (i + 1) * qr
            sums = []
            for rb in blocks:
                top = jnp.max(mt[i][rb], axis=1, keepdims=True)
                e = jnp.exp2((sb[i][rb, 0:width] - top) * scale)
                sums.append(jnp.sum(e, axis=1, keepdims=True))
                e = e.astype(BF)
                for g in range(width // 128):
                    pb[i, rb.start // 16:rb.stop // 16, g] = e[:, g * 128:(g + 1) * 128].reshape(block // 16, 16, 128)
            p = jnp.concatenate([pb[i, :, g].reshape(qr, 128) for g in range(width // 128)], axis=1)
            o = jnp.dot(p, vc[h, 0:width, :], preferred_element_type=F32)
            for rb, total in zip(blocks, sums):
                first = (i * qr + rb.start) // 16
                hbuf[first:first + block // 16, f // 128 + h] = (o[rb] / total).astype(BF).reshape(block // 16, 16, 128)

        for tiles in range(1, per_seq + 1):
            @pl.when(j == tiles - 1)
            def _(tiles=tiles):
                scores(0, 0, tiles)

                @pl.loop(0, hl)
                def _(h):
                    scores(h, 1, tiles)
                    output(h, 0, tiles)
                    scores(jnp.minimum(h + 1, hl - 1), 0, tiles)
                    output(h, 1, tiles)

    def gelu(r):
        return 0.5 * r * (1.0 + lax.erf(r * (0.5 ** 0.5)))

    start(wload("q0", 0))
    xload(0, 0).start()
    if COMM:
        barrier = pltpu.get_barrier_semaphore()
        for dev in (partner, right, left):
            pl.semaphore_signal(barrier, inc=1, device_id=dev, device_id_type=pl.DeviceIdType.MESH)
        pl.semaphore_wait(barrier, 3)

    @pl.loop(0, 4)
    def _(i):
        @pl.when(i < 3)
        def _():
            xload(0, i + 1).start()
        xload(0, i).wait()
        norm(i)

    @pl.loop(0, chunks)
    def _(c):
        n0 = c * nk - 4
        nxt = jnp.minimum(c + 1, chunks - 1)

        wait(wload("q0", 0))
        start(wload("q1", 1))

        def q0():
            put_qkv(c, jnp.dot(gather(ln), wbuf[0, 0:d, 0:qa], preferred_element_type=F32), 0)
        step(n0, q0)

        wait(wload("q1", 1))
        start(wload("g", 0, 0))

        def q1():
            put_qkv(c, jnp.dot(gather(ln), wbuf[1, 0:d, 0:qw - qa], preferred_element_type=F32), qa)
        step(n0 + 1, q1)

        attend(c)

        @pl.loop(0, 2)
        def _(i):
            wait(wload("g", i, i))

            @pl.when(i == 0)
            def _():
                start(wload("g", 1, 1))

            @pl.when(i == 1)
            def _():
                start(wload("d", 0, 0))
                xload(nxt, 0).start()

            def g():
                r = jnp.dot(gather(ln), wbuf[i, 0:d, 0:gw], preferred_element_type=F32)
                scatter(hbuf, i * (gw // 128), gelu(r).astype(BF))
            step(n0 + 2 + i, g)

        @pl.loop(0, 4)
        def _(i):
            slot = lax.rem(i, 2)
            wait(wload("d", slot, i))
            xload(nxt, i).wait()

            @pl.when(i < 3)
            def _():
                start(wload("d", 1 - slot, i + 1))
                xload(nxt, i + 1).start()

            @pl.when(jnp.logical_and(i == 3, c < chunks - 1))
            def _():
                start(wload("q0", 0))

            def dd():
                norm(i)
                r = jnp.dot(gather(hbuf), wbuf[slot, 0:f + hd, 0:dw], preferred_element_type=F32)
                b = c * nk + 2 * i
                part[ring(b)] = r[:, 0:nb].astype(BF)
                part[ring(b + 1)] = r[:, nb:2 * nb].astype(BF)
            step(n0 + 4 + i, dd)

    if COMM:
        @pl.loop(nblk - 4, nblk + LAST)
        def _(n):
            def on(b, g):
                guarded(b < nblk, b, g)
            waits(n, on)
            for delta, f_ in ((1, sum_pair), (3, sum_first), (5, sum_second)):
                on(n - delta, lambda b, f_=f_, w=2 if delta == 1 else DEPTH: f_(b, ring(b), lax.rem(b, w)))
            sends(n, on)


def layer(cfg, x, gamma, beta, wqkv, wo, w1, w2):
    (ntok, d, s, hl, dh, f, tc, tp) = cfg
    nb, to = d // 8, tc // tp
    any_ = pl.BlockSpec(memory_space=pl.ANY)
    vm = pl.BlockSpec(memory_space=pltpu.VMEM)
    qw = 3 * hl * dh
    qa = (qw // 2 + 255) // 256 * 256
    width = max(qa, qw - qa, f // 2, d // 4)
    depth = max(d, f + hl * dh)
    return pl.pallas_call(
        functools.partial(kernel, cfg),
        out_shape=jax.ShapeDtypeStruct((ntok, d), BF),
        in_specs=[any_, vm, vm, any_, any_, any_, any_],
        out_specs=any_,
        scratch_shapes=[
            pltpu.VMEM((2, depth, width), BF),
            pltpu.VMEM((tc // 16, d // 128, 16, 128), BF),
            pltpu.VMEM((hl, tc, dh), BF),
            pltpu.VMEM((hl, s, dh), BF),
            pltpu.VMEM((hl, s, dh), BF),
            pltpu.VMEM((tc // 16, (f + hl * dh) // 128, 16, 128), BF),
            pltpu.VMEM((RING, tc, nb), BF),
            pltpu.VMEM((2, tc // 4, d), BF),
            pltpu.VMEM((tc // 2, s), F32),
            pltpu.VMEM((tc // 2, s), F32),
            pltpu.VMEM((2, tc // 32, s // 128, 16, 128), BF),
            *[pltpu.VMEM((tc // 2, 128), F32) for _ in range(2)],
            pltpu.VMEM((3, tc // 2, nb), BF),
            pltpu.VMEM((DEPTH + 1, to // 2, nb), BF),
            pltpu.VMEM((DEPTH + 1, to // 2, nb), BF),
            pltpu.VMEM((DEPTH + 1, to, nb), BF),
            pltpu.VMEM((DEPTH + 1, to, nb), BF),
            pltpu.VMEM((DEPTH, to, nb), BF),
            pltpu.VMEM((DEPTH + 1, to, nb), BF),
            pltpu.SemaphoreType.DMA((2, 2)),
            pltpu.SemaphoreType.DMA((2,)),
            pltpu.SemaphoreType.DMA((CHANNELS, DEPTH)),
            pltpu.SemaphoreType.DMA((CHANNELS, DEPTH)),
            pltpu.SemaphoreType.DMA((DEPTH,)),
            pltpu.SemaphoreType.DMA((DEPTH,)),
        ],
        compiler_params=pltpu.CompilerParams(
            collective_id=0 if COMM else None, has_side_effects=True, vmem_limit_bytes=67043328),
        name="layer",
    )(x, gamma, beta, wqkv, wo, w1, w2)


def solution(mesh):
    tp = mesh.shape["tp"]

    def local(x, gamma, beta, wqkv, wo, w1, w2):
        b, s, d = x.shape
        hl, dh, _ = wo.shape
        cfg = (b * s, d, s, hl, dh, w1.shape[1], s // 4, tp)
        y = layer(cfg, x.reshape(b * s, d), gamma.reshape(1, d), beta.reshape(1, d),
                  wqkv, wo.reshape(hl * dh, d), w1, w2)
        return y.reshape(b, s, d)

    return jax.shard_map(local, mesh=mesh,
                         in_specs=(P('dp', None, None), P(None), P(None), P(None, 'tp'),
                                   P('tp', None, None), P(None, 'tp'), P('tp', None)),
                         out_specs=P('dp', None, None), check_vma=False)
```

time: 2490 us -> 1180 us (0.47)
  matrix products: 1190 us -> 0 us
  Pallas kernels: 0 us -> 1120 us
  waiting for transfers between devices: 808 us -> 0 us
  other arithmetic: 320 us -> 0 us
  local copies, waits for them, and re-layouts: 149 us -> 55.3 us
    dot_general x12 -> x0, matrix products: 1190 us -> none  [the longest x1 397 us: local(): jnp.dot(hmid, w2, preferred_element_type=jnp.float32)]
    pallas_call x0 -> x1, Pallas kernels: none -> 1120 us  [layer(): pl.pallas_call(functools.partial(kernel, cfg), out_shape=jax.ShapeDtypeSt...]
    psum x1 -> x0, waiting for transfers between devices: 808 us -> none  [local(): total = lax.psum(part_sum, 'tp')]
    reduce_sum x6 -> x0, other arithmetic: 167 us -> none  [the longest x4 111 us: attend(): p = jax.nn.softmax(sc, axis=-1).astype(jnp.bfloat16)]
    convert_element_type x2 -> x0, other arithmetic: 136 us -> none  [the longest x1 80.7 us: local(): (x.astype(jnp.float32) + total.astype(jnp.float32).reshape(b, s, d)).asty...]
    reshape x1 -> x0, local copies, waits for them, and re-layouts: 75.7 us -> none  [local(): qkv.reshape(b, s, gl, hpg + 2, dh)]
    unnamed x4 -> x1, local copies, waits for them, and re-layouts: 0.01 us -> 55.3 us
    squeeze x4 -> x0, local copies, waits for them, and re-layouts: 28.4 us -> none  [local(): lax.map(functools.partial(attend, hpg=hpg), qkv.reshape(b, s, gl, hpg + 2...]
  transfers between devices with their start and end apart: 1 -> 0, of which waited for: 1 -> 0; matrix products, arithmetic and copies ran while one was open for 0% -> 0% of each run, Pallas kernels for 0% -> 0%
where the time goes in v1:
time: 1180 us
  Pallas kernels  1120 us (95%)
  local copies, waits for them, and re-layouts  55.3 us (5%)
    pallas_call x1, Pallas kernels, layer(): pl.pallas_call(functools.partial(kernel, cfg), out_shape=jax.ShapeDtypeSt...  1120 us
    unnamed x1, local copies, waits for them, and re-layouts  55.3 us

profile of v1, /device:TPU:112, one launch (start us, length us, event | category | flops | bytes accessed | tf_op | source)
XLA Modules:
  0.0 1179.8 jit_solution(15462617018084586907)
XLA Ops:
  0.0 1124.5 %layer.1 = bf16[8192,5120]{1,0:T(8,128)(2,1)} custom-call(bf16[8192,5120]{1,0:T(8,128)(2,1)} %bitcast.x, f32[1,5120]{1,0:T(1,128)} %bitcast.6, f32[1,5120]{1,0:T(1,128)} %bitcast.7, bf16[5120,1920]{1,0:T(8,128)(2,1)} %wqkv.1, bf16[640,5120]{1,0:T(8,128)(2,1)} %bitcast.5, bf16[5120,2560]{1,0:T(8,128)(2,1)} %w1.1, bf16[2560,5120]{1,0:T(8,128)(2,1)} %w2.1), custom_call_target="tpu_custom_call" | custom-call | tf_op jit(solution)/shard_map/layer/pallas_call | solution.py:364
  1124.5 55.3 %copy.9 = bf16[4,2048,5120]{2,1,0:T(8,128)(2,1)} copy(bf16[4,2048,5120]{2,1,0:T(8,128)(2,1)} %bitcast.4) | data formatting | bytes 167772160
